TPU v7x, 32 devices: a whole 2x2x4 slice. The times are simulated.
32 devices in a mesh: grp: 2 (over x), mem: 16 (over z, y, core).
Axes of the slice: x: 2, y: 2, z: 4, core: 2. Of those that a mesh axis runs over, the one named last changes fastest.
Arguments:
- phi_owned: float32 [8, 8, 8, 4096], P(None, None, None, ('grp', 'mem')), may hold values from -6 to 6
- band_counts: int32 [2, 16], P('grp'), may hold values from 1 to 128, 512 in all within a row
- neighbours: int32 [2, 6, 512], P('grp'), may hold values from -1 to 1023, as said below
Outputs:
- phi_new: float32 [8, 8, 8, 4096], P(None, None, None, ('grp', 'mem'))
Inputs may be any that keep to these rules, and one draw needn't show every extreme that they name: `band_counts`: in every group the counts sum to 512, each is at least 1, and the largest is exactly 128. `neighbours`: tile k of a group lies at column k mod 16 and row k // 16 of the group's tile sheet. An entry is -1 (no neighbour) or the id of the tile across that face: tile k - 1, k + 1, k - 16, k + 16 of the same group for faces 0 to 3 (never across an edge of the sheet), tile k of group g - 1 or g + 1 for faces 4 and 5. Links are mutual.
All inputs are finite; a program needn't handle non-finite values.
Results may differ from a plain program's by a relative error of at most 0.0003.
Values sent between devices are 32-bit elements; how exact they have to be, the bound alone decides.
A program may use at most 64 MiB of HBM per device.

v0:
```python
import functools

import jax
import jax.numpy as jnp
from jax import lax
from jax.experimental import pallas as pl
from jax.experimental.pallas import tpu as pltpu
from jax.sharding import PartitionSpec as P

STEPS = 4
TIME_STEP = 0.5
EPSILON = 1e-06
LANES = 128
F32 = jnp.float32


def roll(x, shift, axis):
    shift = shift % x.shape[axis]
    return x if shift == 0 else pltpu.roll(x, shift, axis)


def dot(a, b, dims):
    return lax.dot_general(
        a, b, (dims, ((), ())), precision=lax.Precision.HIGHEST, preferred_element_type=F32
    )


def kernel(
    columns, groups, phi_ref, counts_ref, links_ref, out_ref,
    leave, land, back, home, up, down, from_below, from_above, right, left, from_left, from_right,
    level, sign, out_send, out_recv, back_send, back_recv, side_send, side_recv,
):
    edge = phi_ref.shape[0]
    own_slots = phi_ref.shape[3]
    padded, tiles = leave.shape[1], links_ref.shape[2]
    rows = tiles // columns
    halo = STEPS
    wide = 2 * edge
    layers = edge + 2 * halo
    me, grp = lax.axis_index("mem"), lax.axis_index("grp")
    has_left, has_right = me > 0, me < columns - 1
    has_below, has_above = grp > 0, grp < groups - 1

    for ref in (from_below, from_above, from_left, from_right):
        ref[...] = jnp.zeros_like(ref)

    barrier = pltpu.get_barrier_semaphore()
    for d in range(1, columns):
        pl.semaphore_signal(barrier, inc=1, device_id={"mem": lax.rem(me + d, columns)},
                            device_id_type=pl.DeviceIdType.MESH)

    @pl.when(has_below)
    def _():
        pl.semaphore_signal(barrier, inc=1, device_id={"grp": grp - 1},
                            device_id_type=pl.DeviceIdType.MESH)

    @pl.when(has_above)
    def _():
        pl.semaphore_signal(barrier, inc=1, device_id={"grp": grp + 1},
                            device_id_type=pl.DeviceIdType.MESH)

    def exchange(source, target, send, recv):
        started = []
        for d in range(1, columns):
            peer = lax.rem(me + d, columns)
            copy = pltpu.make_async_remote_copy(
                src_ref=source.at[peer], dst_ref=target.at[me],
                send_sem=send.at[d], recv_sem=recv.at[d],
                device_id={"mem": peer}, device_id_type=pl.DeviceIdType.MESH)
            copy.start()
            started.append(copy)
        target[me] = source[me]
        for d in range(1, columns):
            origin = lax.rem(me + columns - d, columns)
            pltpu.make_async_remote_copy(
                src_ref=source.at[origin], dst_ref=target.at[origin],
                send_sem=send.at[d], recv_sem=recv.at[d],
                device_id={"mem": origin}, device_id_type=pl.DeviceIdType.MESH).wait_recv()
        return started

    def shift_copy(source, target, index, axis, peer):
        return pltpu.make_async_remote_copy(
            src_ref=source, dst_ref=target, send_sem=side_send.at[index],
            recv_sem=side_recv.at[index], device_id={axis: peer},
            device_id_type=pl.DeviceIdType.MESH)

    def both_ways(axis, here, more, less, ahead, behind, target_of_ahead, target_of_behind, base):
        to_ahead = shift_copy(ahead, target_of_ahead, base, axis, here + 1)
        to_behind = shift_copy(behind, target_of_behind, base + 1, axis, here - 1)
        pl.when(more)(to_ahead.start)
        pl.when(less)(to_behind.start)
        late.extend([(more, to_ahead), (less, to_behind)])

        def arrived():
            pl.when(less)(to_ahead.wait_recv)
            pl.when(more)(to_behind.wait_recv)

        return arrived

    late = []

    count_of = [counts_ref[0, m] for m in range(columns)]
    first, count = jnp.int32(0), jnp.int32(0)
    for m in range(columns):
        first = first + jnp.where(m < me, count_of[m], 0)
        count = count + jnp.where(m == me, count_of[m], 0)
    entries = columns * padded
    slot = lax.broadcasted_iota(jnp.int32, (1, own_slots), 1)
    key = (first + slot) % columns * padded + slot // columns
    chosen = lax.broadcasted_iota(jnp.int32, (entries, own_slots), 0) == key
    placing = jnp.where(chosen, 1.0, 0.0).astype(F32)
    entry = lax.broadcasted_iota(jnp.int32, (1, entries), 1)
    block, place = entry // padded, entry % padded
    start, length = jnp.zeros((1, entries), jnp.int32), jnp.zeros((1, entries), jnp.int32)
    for m in range(columns):
        start = start + jnp.where(block > m, count_of[m], 0)
        length = length + jnp.where(block == m, count_of[m], 0)
    offset = lax.broadcasted_iota(jnp.int32, (rows, entries), 0) * columns + me - start
    begin = place * columns
    arrive = jnp.where((offset >= begin) & (offset < begin + columns) & (offset < length),
                       1.0, 0.0).astype(F32)

    cells = jnp.concatenate(
        [phi_ref[2 * pair + k, y] for pair in range(edge // 2) for y in range(edge) for k in range(2)],
        axis=0)
    leave[...] = dot(placing, cells, ((1,), (1,))).reshape(leave.shape)

    held = (lax.broadcasted_iota(jnp.int32, (rows, tiles), 0) * columns + me
            == lax.broadcasted_iota(jnp.int32, (rows, tiles), 1))

    def link(face):
        there = jnp.where(links_ref[face] >= 0, 1.0, 0.0).astype(F32)
        value = jnp.sum(jnp.where(held, there, 0.0), axis=1, keepdims=True)
        return jnp.broadcast_to(value, (rows, LANES))

    link_x = [link(0), link(1)]
    link_y = link(2)
    link_z = [link(4), link(5)]
    lane = lax.broadcasted_iota(jnp.int32, (rows, LANES), 1)
    z = lane % wide

    pl.semaphore_wait(barrier, columns - 1 + has_below.astype(jnp.int32) + has_above.astype(jnp.int32))
    sent = exchange(leave, land, out_send, out_recv)

    packed = dot(arrive, land[...].reshape(-1, land.shape[2]), ((1,), (0,)))
    mine = []
    for pair in range(edge // 2):
        both = packed[:, pair * LANES:(pair + 1) * LANES]
        mine += [roll(both, halo, 1), roll(both, halo - edge, 1)]

    parts = mine + [link_y] + link_x
    slots = up.shape[0]
    for q in range(slots):
        high, low = jnp.zeros((rows, LANES), F32), jnp.zeros((rows, LANES), F32)
        for k in range(4):
            if 4 * q + k < len(parts):
                inside = (z >= halo * k) & (z < halo * (k + 1))
                part = parts[4 * q + k]
                high = jnp.where(inside, roll(part, halo * k - edge, 1), high)
                low = jnp.where(inside, roll(part, halo * k - halo, 1), low)
        up[q] = high
        down[q] = low
    both_ways("grp", grp, has_above, has_below, up, down, from_below, from_above, 0)()

    filled = []
    for i, part in enumerate(parts):
        q, k = divmod(i, 4)
        below = roll(from_below[q], -halo * k, 1)
        above = roll(from_above[q], halo + edge - halo * k, 1)
        filled.append(jnp.where(z < halo, below, jnp.where(z >= halo + edge, above, part)))
    mine, link_y, link_x = filled[:edge], filled[edge], filled[edge + 1:]
    link_z = jnp.where(z == halo, link_z[0], jnp.where(z == halo + edge, link_z[1],
                       jnp.where(z == 0, 0.0, 1.0)))
    link_y = jnp.where(lane < wide, link_y, 1.0)

    for k in range(halo):
        right[k] = mine[edge - halo + k]
        left[k] = mine[k]
    for ref in (right, left):
        ref[halo] = link_y
        ref[halo + 1] = link_z
    arrived = both_ways("mem", me, has_right, has_left, right, left, from_left, from_right, 2)

    masks_y, masks_z = [None, link_y, None], [None, link_z, None]

    def begin_layer(i, value):
        level[0, i] = value
        sign[i] = value / jnp.sqrt(value * value + 1.0)

    def sweep(step, low, high):
        now, later = step % 2, (step + 1) % 2
        gap = None
        for i in range(low, high):
            region = 0 if i < halo else (1 if i < halo + edge else 2)
            mask_y, mask_z = masks_y[region], masks_z[region]
            value, field = level[now, i], sign[i]
            side = jnp.where(field > 0, 1.0, -1.0)

            def across(j):
                change = level[now, j] - level[now, j - 1]
                if j == halo:
                    change = change * link_x[0]
                elif j == halo + edge:
                    change = change * link_x[1]
                return change

            gap = across(i) if gap is None else gap
            ahead = across(i + 1)
            most = jnp.maximum(jnp.maximum(side * gap, -(side * ahead)), 0.0)
            squares = most * most
            gap = ahead

            turned = roll(value, wide, 1)
            before = jnp.where(lane < wide, roll(turned, 1, 0), turned)
            behind = (value - before) * mask_y
            turned = roll(behind, -wide, 1)
            ahead = jnp.where(lane >= LANES - wide, roll(turned, -1, 0), turned)
            most = jnp.maximum(jnp.maximum(side * behind, -(side * ahead)), 0.0)
            squares = squares + most * most

            behind = (value - roll(value, 1, 1)) * mask_z
            ahead = roll(behind, -1, 1)
            most = jnp.maximum(jnp.maximum(side * behind, -(side * ahead)), 0.0)
            squares = squares + most * most
            level[later, i] = value - TIME_STEP * field * (jnp.sqrt(squares + EPSILON) - 1.0)

    for i in range(edge):
        begin_layer(halo + i, mine[i])
    sweep(0, halo + 1, halo + edge - 1)
    arrived()
    masks_y[0], masks_y[2] = from_left[halo], from_right[halo]
    masks_z[0], masks_z[2] = from_left[halo + 1], from_right[halo + 1]
    for i in range(halo):
        begin_layer(i, from_left[i])
        begin_layer(halo + edge + i, from_right[i])
    sweep(0, 1, halo + 1)
    sweep(0, halo + edge - 1, layers - 1)
    for step in range(1, STEPS):
        sweep(step, step + 1, layers - 1 - step)

    last = STEPS % 2
    pairs = []
    for pair in range(edge // 2):
        first, second = level[last, halo + 2 * pair], level[last, halo + 2 * pair + 1]
        pairs.append(jnp.where(z < edge, roll(first, -halo, 1), roll(second, edge - halo, 1)))
    final = jnp.concatenate(pairs, axis=1)
    back[...] = dot(arrive, final, ((0,), (0,))).reshape(back.shape)
    sent += exchange(back, home, back_send, back_recv)

    living = jnp.where(slot < count, placing, 0.0)
    owned = dot(living, home[...].reshape(-1, home.shape[2]), ((0,), (0,))).T
    for pair in range(edge // 2):
        for y in range(edge):
            for k in range(2):
                at = ((pair * edge + y) * 2 + k) * edge
                out_ref[2 * pair + k, y] = owned[at:at + edge]
    for copy in sent:
        copy.wait_send()
    for there, copy in late:
        pl.when(there)(copy.wait_send)


def on_device(phi_owned, band_counts, neighbours):
    edge, own_slots = phi_owned.shape[0], phi_owned.shape[3]
    columns, groups = lax.axis_size("mem"), lax.axis_size("grp")
    rows = neighbours.shape[2] // columns
    padded = -(-own_slots // (8 * columns)) * 8
    halo, cells = STEPS, edge * edge * edge
    vmem = pl.BlockSpec(memory_space=pltpu.VMEM)
    buffer = pltpu.VMEM((columns, padded, cells), F32)
    strip = pltpu.VMEM((-(-(edge + 3) // 4), rows, LANES), F32)
    face = pltpu.VMEM((halo + 2, rows, LANES), F32)
    layers = edge + 2 * halo
    return pl.pallas_call(
        functools.partial(kernel, columns, groups),
        out_shape=jax.ShapeDtypeStruct(phi_owned.shape, F32),
        in_specs=[vmem, pl.BlockSpec(memory_space=pltpu.SMEM), vmem],
        out_specs=vmem,
        scratch_shapes=[buffer] * 4 + [strip] * 4 + [face] * 4 + [
            pltpu.VMEM((2, layers, rows, LANES), F32),
            pltpu.VMEM((layers, rows, LANES), F32),
        ] + [pltpu.SemaphoreType.DMA((columns,))] * 4 + [pltpu.SemaphoreType.DMA((4,))] * 2,
        compiler_params=pltpu.CompilerParams(collective_id=0, has_side_effects=True),
    )(phi_owned, band_counts, jnp.transpose(neighbours, (1, 0, 2)))


def solution(mesh):
    return jax.shard_map(
        on_device,
        mesh=mesh,
        in_specs=(P(None, None, None, ("grp", "mem")), P("grp", None), P("grp", None, None)),
        out_specs=P(None, None, None, ("grp", "mem")),
        check_vma=False,
    )
```

profile of v0, /device:TPU:13, one launch (start us, length us, event | category | flops | bytes accessed | tf_op | source)
XLA Modules:
  0.0 31.8 jit_solution(11414870456637471310)
XLA Ops:
  0.0 30.1 %shard_map.37 = f32[8,8,8,128]{3,2,1,0:T(8,128)} custom-call(f32[8,8,8,128]{3,2,1,0:T(8,128)} %phi_ref.1, s32[1,16]{1,0:T(1,128)} %counts_ref.1, s32[6,1,512]{2,1,0:T(1,128)} %bitcast.1), custom_call_target="tpu_custom_call" | custom-call | tf_op jit(solution)/shard_map/pallas_call | solution.py:274
  30.2 1.7 %copy.5 = f32[8,8,8,128]{3,2,1,0:T(8,128)} copy(f32[8,8,8,128]{3,2,1,0:T(8,128)} %shard_map.37) | data formatting | bytes 524288
where the time goes:
time: 32 us; the launch traced here: 31.8 us
  Pallas kernels  30.1 us (94%)
  local copies, waits for them, and re-layouts  1.67 us (5%)
    pallas_call x1, Pallas kernels, on_device(): pl.pallas_call(functools.partial(kernel, columns, groups), out_shape=jax....  30.1 us
    unnamed x1, local copies, waits for them, and re-layouts  1.67 us

commit v1 on v0

v1 whole, which is shorter than its diff:
```python
import functools

import jax
import jax.numpy as jnp
from jax import lax
from jax.experimental import pallas as pl
from jax.experimental.pallas import tpu as pltpu
from jax.sharding import PartitionSpec as P

STEPS = 4
TIME_STEP = 0.5
EPSILON = 1e-06
LANES = 128
F32 = jnp.float32
BF16 = jnp.bfloat16


def roll(x, shift, axis):
    shift = shift % x.shape[axis]
    return x if shift == 0 else pltpu.roll(x, shift, axis)


def pieces(x, axis):
    high = x.astype(BF16)
    rest = x - high.astype(F32)
    middle = rest.astype(BF16)
    low = (rest - middle.astype(F32)).astype(BF16)
    return jnp.concatenate([high, middle, low], axis=axis)


def dot(a, b, dims):
    return lax.dot_general(a, b, (dims, ((), ())), preferred_element_type=F32)


def kernel(
    columns, groups, phi_hbm, counts_hbm, links_hbm, out_ref,
    phi_ref, counts_ref, links_own, links_below, links_above,
    leave, land, back, home, pack, up, down, from_below, from_above, from_left, from_right,
    level, sign, in_sem, out_send, out_recv, back_send, back_recv, side_send, side_recv,
):
    edge = phi_ref.shape[0]
    own_slots = phi_ref.shape[3]
    padded, tiles = leave.shape[1], links_own.shape[2]
    rows = tiles // columns
    halo = STEPS
    wide = 2 * edge
    layers = edge + 2 * halo
    me, grp = lax.axis_index("mem"), lax.axis_index("grp")
    has_left, has_right = me > 0, me < columns - 1
    has_below, has_above = grp > 0, grp < groups - 1
    across_grp = [(-1, has_below), (1, has_above)]
    across_mem = [(-1, has_left), (1, has_right)]
    distances = sorted(range(1, columns), key=lambda d: -min(d, columns - d))

    fetch = [
        pltpu.make_async_copy(phi_hbm, phi_ref, in_sem.at[0]),
        pltpu.make_async_copy(counts_hbm, counts_ref, in_sem.at[1]),
        pltpu.make_async_copy(links_hbm, links_own, in_sem.at[2]),
    ]
    for copy in fetch:
        copy.start()
    for ref in (from_below, from_above, from_left, from_right):
        ref[...] = jnp.zeros_like(ref)
    for ref in (links_below, links_above):
        ref[...] = jnp.full_like(ref, -1)

    barrier = pltpu.get_barrier_semaphore()

    def greet(**peer):
        pl.semaphore_signal(barrier, inc=1, device_id=peer, device_id_type=pl.DeviceIdType.MESH)

    for d in distances:
        greet(mem=lax.rem(me + d, columns))
    greetings = jnp.int32(columns - 1)
    for dg, there in across_grp:
        for dm, beside in across_mem + [(0, True)]:
            both = jnp.logical_and(there, beside)
            greetings = greetings + both.astype(jnp.int32)

            @pl.when(both)
            def _():
                greet(grp=grp + dg, mem=me + dm)

    def remote(source, target, send, recv, **peer):
        return pltpu.make_async_remote_copy(
            src_ref=source, dst_ref=target, send_sem=send, recv_sem=recv,
            device_id=peer, device_id_type=pl.DeviceIdType.MESH)

    def begin_exchange(source, target, send, recv):
        started = []
        for d in distances:
            peer = lax.rem(me + d, columns)
            copy = remote(source.at[peer], target.at[me], send.at[d], recv.at[d], mem=peer)
            copy.start()
            started.append(copy)
        target[me] = source[me]
        return started

    def end_exchange(source, target, send, recv):
        for d in reversed(distances):
            origin = lax.rem(me + columns - d, columns)
            remote(source.at[origin], target.at[origin], send.at[d], recv.at[d],
                   mem=origin).wait_recv()

    late = []

    def shift(index, condition, sources, copy):
        pl.when(condition)(copy.start)
        late.append((condition, copy))
        return lambda: pl.when(sources)(copy.wait_recv)

    fetch[1].wait()
    count_of = [counts_ref[0, m] for m in range(columns)]
    first, count = jnp.int32(0), jnp.int32(0)
    for m in range(columns):
        first = first + jnp.where(m < me, count_of[m], 0)
        count = count + jnp.where(m == me, count_of[m], 0)
    entries = columns * padded
    slot = lax.broadcasted_iota(jnp.int32, (1, own_slots), 1)
    key = (first + slot) % columns * padded + slot // columns
    chosen = lax.broadcasted_iota(jnp.int32, (entries, own_slots), 0) == key
    placing = jnp.where(chosen, 1.0, 0.0).astype(F32)

    fetch[0].wait()
    cells = jnp.concatenate(
        [phi_ref[2 * pair + k, y] for pair in range(edge // 2) for y in range(edge) for k in range(2)],
        axis=0)
    leave[...] = dot(jnp.concatenate([placing.astype(BF16)] * 3, axis=1), pieces(cells, 1),
                     ((1,), (1,))).reshape(leave.shape)
    fetch[2].wait()

    pl.semaphore_wait(barrier, greetings)
    sent = begin_exchange(leave, land, out_send, out_recv)
    tables = [
        shift(0, has_above, has_below, remote(
            links_own, links_below, side_send.at[0], side_recv.at[0], grp=grp + 1)),
        shift(1, has_below, has_above, remote(
            links_own, links_above, side_send.at[1], side_recv.at[1], grp=grp - 1)),
    ]

    def arrival(dims, axis):
        entry = lax.broadcasted_iota(jnp.int32, dims, axis)
        block, place = entry // padded, entry % padded
        start, length = jnp.zeros(dims, jnp.int32), jnp.zeros(dims, jnp.int32)
        for m in range(columns):
            start = start + jnp.where(block > m, count_of[m], 0)
            length = length + jnp.where(block == m, count_of[m], 0)
        shape = (rows, entries) if axis == 1 else (entries, rows)
        offset = lax.broadcasted_iota(jnp.int32, shape, 1 - axis) * columns + me - start
        begin = place * columns
        return jnp.where((offset >= begin) & (offset < begin + columns) & (offset < length),
                         1.0, 0.0).astype(F32).astype(BF16)

    arrive = jnp.concatenate([arrival((1, entries), 1)] * 3, axis=1)
    depart = jnp.concatenate([arrival((entries, 1), 0)] * 3, axis=1)
    living = jnp.concatenate([jnp.where(slot < count, placing, 0.0).astype(BF16)] * 3, axis=0)

    lane = lax.broadcasted_iota(jnp.int32, (rows, LANES), 1)
    z = lane % wide
    tile_of = (lax.broadcasted_iota(jnp.int32, (rows, tiles), 1)
               - lax.broadcasted_iota(jnp.int32, (rows, tiles), 0) * columns - me)
    held = {dm: tile_of == dm for dm in (-1, 0, 1)}

    for arrived in tables:
        arrived()

    def link(table, face, dm):
        there = jnp.where(table[face] >= 0, 1.0, 0.0).astype(F32)
        value = jnp.sum(jnp.where(held[dm], there, 0.0), axis=1, keepdims=True)
        return jnp.broadcast_to(value, (rows, LANES))

    def layered(face, dm):
        return jnp.where(z < halo, link(links_below, face, dm),
                         jnp.where(z >= halo + edge, link(links_above, face, dm),
                                   link(links_own, face, dm)))

    link_x = [layered(0, 0), layered(1, 0)]
    masks_y = [jnp.where(lane < wide, layered(2, dm), 1.0) for dm in (-1, 0, 1)]
    masks_z = [jnp.where(z == halo, link(links_own, 4, dm),
                         jnp.where(z == halo + edge, link(links_own, 5, dm),
                                   jnp.where(z == 0, 0.0, 1.0))) for dm in (-1, 0, 1)]

    end_exchange(leave, land, out_send, out_recv)
    packed = dot(arrive, pieces(land[...].reshape(-1, land.shape[2]), 0), ((1,), (0,)))
    pairs = [packed[:, p * LANES:(p + 1) * LANES] for p in range(edge // 2)]
    for p, both in enumerate(pairs):
        pack[p] = both
    low = lane % edge < halo
    slots = up.shape[0]
    for q in range(slots):
        here, after = pairs[2 * q], pairs[2 * q + 1]
        up[q] = jnp.where(low, roll(after, -halo, 1), here)
        down[q] = jnp.where(low, here, roll(after, halo, 1))

    half = edge // 4
    messages = []
    for dg, there, back_there, source, target, base in (
        (1, has_above, has_below, up, from_below, 2), (-1, has_below, has_above, down, from_above, 5),
    ):
        for k, (dm, beside, back_beside, part) in enumerate((
            (1, has_right, has_left, slots - 1), (-1, has_left, has_right, 0),
        )):
            messages.append(shift(
                base + k, jnp.logical_and(there, beside), jnp.logical_and(back_there, back_beside),
                remote(source.at[part], target.at[1 - dm, part], side_send.at[base + k],
                       side_recv.at[base + k], grp=grp + dg, mem=me + dm)))
        messages.append(shift(
            base + 2, there, back_there,
            remote(source, target.at[1], side_send.at[base + 2], side_recv.at[base + 2], grp=grp + dg)))
    messages.append(shift(8, has_right, has_left, remote(
        pack.at[pl.ds(half, half)], from_left, side_send.at[8], side_recv.at[8], mem=me + 1)))
    messages.append(shift(9, has_left, has_right, remote(
        pack.at[pl.ds(0, half)], from_right, side_send.at[9], side_recv.at[9], mem=me - 1)))

    for arrived in messages:
        arrived()

    for i in range(layers):
        x = i - halo
        region = 0 if x < 0 else (1 if x < edge else 2)
        x = x % edge
        p, k = divmod(x, 2)
        q, t = divmod(p, 2)
        own = pairs[p] if region == 1 else (from_left[p - half] if region == 0 else from_right[p])
        below = roll(from_below[region, q], -halo * (1 - t) - edge * k, 1)
        above = roll(from_above[region, q], edge + halo - edge * k - halo * t, 1)
        value = jnp.where(z < halo, below,
                          jnp.where(z >= halo + edge, above, roll(own, halo - edge * k, 1)))
        level[0, i] = value
        sign[i] = value / jnp.sqrt(value * value + 1.0)

    def sweep(step, low, high):
        now, later = step % 2, (step + 1) % 2
        gap = None
        for i in range(low, high):
            region = 0 if i < halo else (1 if i < halo + edge else 2)
            mask_y, mask_z = masks_y[region], masks_z[region]
            value, field = level[now, i], sign[i]
            side = jnp.where(field > 0, 1.0, -1.0)

            def across(j):
                change = level[now, j] - level[now, j - 1]
                if j == halo:
                    change = change * link_x[0]
                elif j == halo + edge:
                    change = change * link_x[1]
                return change

            gap = across(i) if gap is None else gap
            ahead = across(i + 1)
            most = jnp.maximum(jnp.maximum(side * gap, -(side * ahead)), 0.0)
            squares = most * most
            gap = ahead

            turned = roll(value, wide, 1)
            before = jnp.where(lane < wide, roll(turned, 1, 0), turned)
            behind = (value - before) * mask_y
            turned = roll(behind, -wide, 1)
            ahead = jnp.where(lane >= LANES - wide, roll(turned, -1, 0), turned)
            most = jnp.maximum(jnp.maximum(side * behind, -(side * ahead)), 0.0)
            squares = squares + most * most

            behind = (value - roll(value, 1, 1)) * mask_z
            ahead = roll(behind, -1, 1)
            most = jnp.maximum(jnp.maximum(side * behind, -(side * ahead)), 0.0)
            squares = squares + most * most
            level[later, i] = value - TIME_STEP * field * (jnp.sqrt(squares + EPSILON) - 1.0)

    for step in range(STEPS):
        sweep(step, step + 1, layers - 1 - step)

    last = STEPS % 2
    final = []
    for pair in range(edge // 2):
        one, two = level[last, halo + 2 * pair], level[last, halo + 2 * pair + 1]
        final.append(jnp.where(z < edge, roll(one, -halo, 1), roll(two, edge - halo, 1)))
    back[...] = dot(depart, pieces(jnp.concatenate(final, axis=1), 0),
                    ((1,), (0,))).reshape(back.shape)
    sent += begin_exchange(back, home, back_send, back_recv)
    end_exchange(back, home, back_send, back_recv)

    owned = dot(living, pieces(home[...].reshape(-1, home.shape[2]), 0), ((0,), (0,))).T
    for pair in range(edge // 2):
        for y in range(edge):
            for k in range(2):
                at = ((pair * edge + y) * 2 + k) * edge
                out_ref[2 * pair + k, y] = owned[at:at + edge]
    for copy in sent:
        copy.wait_send()
    for there, copy in late:
        pl.when(there)(copy.wait_send)


def on_device(phi_owned, band_counts, neighbours):
    edge, own_slots = phi_owned.shape[0], phi_owned.shape[3]
    columns, groups = lax.axis_size("mem"), lax.axis_size("grp")
    tiles = neighbours.shape[2]
    rows = tiles // columns
    padded = -(-own_slots // (8 * columns)) * 8
    halo, cells = STEPS, edge * edge * edge
    anywhere = pl.BlockSpec(memory_space=pl.ANY)
    buffer = pltpu.VMEM((columns, padded, cells), F32)
    table = pltpu.VMEM((6, 1, tiles), jnp.int32)
    pair = lambda *lead: pltpu.VMEM((*lead, rows, LANES), F32)
    slots, layers = edge // 4, edge + 2 * halo
    return pl.pallas_call(
        functools.partial(kernel, columns, groups),
        out_shape=jax.ShapeDtypeStruct(phi_owned.shape, F32),
        in_specs=[anywhere] * 3,
        out_specs=pl.BlockSpec(memory_space=pltpu.VMEM),
        scratch_shapes=[
            pltpu.VMEM(phi_owned.shape, F32), pltpu.SMEM(band_counts.shape, jnp.int32),
            table, table, table,
        ] + [buffer] * 4 + [
            pair(edge // 2), pair(slots), pair(slots), pair(3, slots), pair(3, slots),
            pair(edge // 4), pair(edge // 4), pair(2, layers), pair(layers),
            pltpu.SemaphoreType.DMA((3,)),
        ] + [pltpu.SemaphoreType.DMA((columns,))] * 4 + [pltpu.SemaphoreType.DMA((10,))] * 2,
        compiler_params=pltpu.CompilerParams(collective_id=0, has_side_effects=True),
    )(phi_owned, band_counts, jnp.transpose(neighbours, (1, 0, 2)))


def solution(mesh):
    return jax.shard_map(
        on_device,
        mesh=mesh,
        in_specs=(P(None, None, None, ("grp", "mem")), P("grp", None), P("grp", None, None)),
        out_specs=P(None, None, None, ("grp", "mem")),
        check_vma=False,
    )
```

time: 32 us -> 30.7 us (0.959)
  the two profiles are of different devices: /device:TPU:13 before, /device:TPU:0 now
where the time goes in v1:
time: 30.7 us; the launch traced here: 30.5 us
  Pallas kernels  28.8 us (94%)
  local copies, waits for them, and re-layouts  1.67 us (5%)
    pallas_call x1, Pallas kernels, on_device(): pl.pallas_call(functools.partial(kernel, columns, groups), out_shape=jax....  28.8 us
    unnamed x1, local copies, waits for them, and re-layouts  1.67 us

profile of v1, /device:TPU:0, one launch (start us, length us, event | category | flops | bytes accessed | tf_op | source)
XLA Modules:
  0.0 30.5 jit_solution(6569864964590421670)
XLA Ops:
  0.0 28.8 %shard_map.37 = f32[8,8,8,128]{3,2,1,0:T(8,128)} custom-call(f32[8,8,8,128]{3,2,1,0:T(8,128)} %phi_hbm.1, s32[1,16]{1,0:T(1,128)} %counts_hbm.1, s32[6,1,512]{2,1,0:T(1,128)} %bitcast.1), custom_call_target="tpu_custom_call" | custom-call | tf_op jit(solution)/shard_map/pallas_call | solution.py:306
  28.8 1.7 %copy.5 = f32[8,8,8,128]{3,2,1,0:T(8,128)} copy(f32[8,8,8,128]{3,2,1,0:T(8,128)} %shard_map.37) | data formatting | bytes 524288

commit v2 on v1

--- a/solution.py
+++ b/solution.py
@@ -50,7 +50,7 @@
     has_below, has_above = grp > 0, grp < groups - 1
     across_grp = [(-1, has_below), (1, has_above)]
     across_mem = [(-1, has_left), (1, has_right)]
-    distances = sorted(range(1, columns), key=lambda d: -min(d, columns - d))
+    distances = range(1, columns)
 
     fetch = [
         pltpu.make_async_copy(phi_hbm, phi_ref, in_sem.at[0]),
@@ -298,7 +298,7 @@
     rows = tiles // columns
     padded = -(-own_slots // (8 * columns)) * 8
     halo, cells = STEPS, edge * edge * edge
-    anywhere = pl.BlockSpec(memory_space=pl.ANY)
+    anywhere = pl.BlockSpec(memory_space=pltpu.HBM)
     buffer = pltpu.VMEM((columns, padded, cells), F32)
     table = pltpu.VMEM((6, 1, tiles), jnp.int32)
     pair = lambda *lead: pltpu.VMEM((*lead, rows, LANES), F32)
@@ -316,8 +316,10 @@
             pair(edge // 4), pair(edge // 4), pair(2, layers), pair(layers),
             pltpu.SemaphoreType.DMA((3,)),
         ] + [pltpu.SemaphoreType.DMA((columns,))] * 4 + [pltpu.SemaphoreType.DMA((10,))] * 2,
-        compiler_params=pltpu.CompilerParams(collective_id=0, has_side_effects=True),
-    )(phi_owned, band_counts, jnp.transpose(neighbours, (1, 0, 2)))
+        compiler_params=pltpu.CompilerParams(
+            collective_id=0, has_side_effects=True, vmem_limit_bytes=16 * 1024 * 1024),
+    )(*[pltpu.with_memory_space_constraint(x, pltpu.HBM)
+        for x in (phi_owned, band_counts, jnp.transpose(neighbours, (1, 0, 2)))])
 
 
 def solution(mesh):

time: 30.7 us -> 26.9 us (0.88)
  Pallas kernels: 28.8 us -> 26.1 us
  local copies, waits for them, and re-layouts: 1.67 us -> 0.71 us
    pallas_call x1, Pallas kernels: 28.8 us -> 26.1 us  [on_device(): pl.pallas_call(functools.partial(kernel, columns, groups), out_shape=jax....]
    unnamed x1, local copies, waits for them, and re-layouts: 1.67 us -> 0.71 us
where the time goes in v2:
time: 26.9 us; the launch traced here: 26.8 us
  Pallas kernels  26.1 us (97%)
  local copies, waits for them, and re-layouts  0.71 us (3%)
    pallas_call x1, Pallas kernels, on_device(): pl.pallas_call(functools.partial(kernel, columns, groups), out_shape=jax....  26.1 us
    unnamed x1, local copies, waits for them, and re-layouts  0.71 us

profile of v2, /device:TPU:0, one launch (start us, length us, event | category | flops | bytes accessed | tf_op | source)
XLA Modules:
  0.0 26.8 jit_solution(13661235503821682489)
XLA Ops:
  0.0 26.1 %shard_map.37 = f32[8,8,8,128]{3,2,1,0:T(8,128)S(1)} custom-call(f32[8,8,8,128]{3,2,1,0:T(8,128)} %phi_hbm.1, s32[1,16]{1,0:T(1,128)} %counts_hbm.1, s32[6,1,512]{2,1,0:T(1,128)} %bitcast.1), custom_call_target="tpu_custom_call" | custom-call | tf_op jit(solution)/shard_map/pallas_call | solution.py:306
  26.1 0.7 %copy.5 = f32[8,8,8,128]{3,2,1,0:T(8,128)} copy(f32[8,8,8,128]{3,2,1,0:T(8,128)S(1)} %shard_map.37) | data formatting | bytes 524288

commit v3 on v2

--- a/solution.py
+++ b/solution.py
@@ -36,7 +36,7 @@
     columns, groups, phi_hbm, counts_hbm, links_hbm, out_ref,
     phi_ref, counts_ref, links_own, links_below, links_above,
     leave, land, back, home, pack, up, down, from_below, from_above, from_left, from_right,
-    level, sign, in_sem, out_send, out_recv, back_send, back_recv, side_send, side_recv,
+    level, sign, turned, in_sem, out_send, out_recv, back_send, back_recv, side_send, side_recv,
 ):
     edge = phi_ref.shape[0]
     own_slots = phi_ref.shape[3]
@@ -227,44 +227,56 @@
         value = jnp.where(z < halo, below,
                           jnp.where(z >= halo + edge, above, roll(own, halo - edge * k, 1)))
         level[0, i] = value
-        sign[i] = value / jnp.sqrt(value * value + 1.0)
+        sign[i] = value * lax.rsqrt(value * value + 1.0)
+
+    always = me < columns
+
+    def row_ahead(x):
+        return jnp.where(lane >= LANES - wide, roll(x, -1, 0), x)
+
+    ahead_y = [row_ahead(roll(mask, -wide, 1)) for mask in masks_y]
+    ahead_z = [roll(mask, -1, 1) for mask in masks_z]
+
+    def steepest(side, behind, ahead):
+        most = jnp.maximum(jnp.maximum(side * behind, -(side * ahead)), 0.0)
+        return most * most
 
     def sweep(step, low, high):
         now, later = step % 2, (step + 1) % 2
-        gap = None
-        for i in range(low, high):
-            region = 0 if i < halo else (1 if i < halo + edge else 2)
-            mask_y, mask_z = masks_y[region], masks_z[region]
-            value, field = level[now, i], sign[i]
-            side = jnp.where(field > 0, 1.0, -1.0)
-
-            def across(j):
-                change = level[now, j] - level[now, j - 1]
-                if j == halo:
-                    change = change * link_x[0]
-                elif j == halo + edge:
-                    change = change * link_x[1]
-                return change
-
-            gap = across(i) if gap is None else gap
-            ahead = across(i + 1)
-            most = jnp.maximum(jnp.maximum(side * gap, -(side * ahead)), 0.0)
-            squares = most * most
-            gap = ahead
-
-            turned = roll(value, wide, 1)
-            before = jnp.where(lane < wide, roll(turned, 1, 0), turned)
-            behind = (value - before) * mask_y
-            turned = roll(behind, -wide, 1)
-            ahead = jnp.where(lane >= LANES - wide, roll(turned, -1, 0), turned)
-            most = jnp.maximum(jnp.maximum(side * behind, -(side * ahead)), 0.0)
-            squares = squares + most * most
-
-            behind = (value - roll(value, 1, 1)) * mask_z
-            ahead = roll(behind, -1, 1)
-            most = jnp.maximum(jnp.maximum(side * behind, -(side * ahead)), 0.0)
-            squares = squares + most * most
-            level[later, i] = value - TIME_STEP * field * (jnp.sqrt(squares + EPSILON) - 1.0)
+
+        @pl.when(always)
+        def _():
+            for k, shift_by in enumerate((wide, -wide, 1, -1)):
+                for i in range(low, high):
+                    turned[k, i] = roll(level[now, i], shift_by, 1)
+
+        @pl.when(always)
+        def _():
+            gap = None
+            for i in range(low, high):
+                region = 0 if i < halo else (1 if i < halo + edge else 2)
+                value, field = level[now, i], sign[i]
+                side = jnp.where(field > 0, 1.0, -1.0)
+
+                def across(j):
+                    change = level[now, j] - level[now, j - 1]
+                    if j == halo:
+                        change = change * link_x[0]
+                    elif j == halo + edge:
+                        change = change * link_x[1]
+                    return change
+
+                gap = across(i) if gap is None else gap
+                ahead = across(i + 1)
+                squares = steepest(side, gap, ahead)
+                gap = ahead
+                before = turned[0, i]
+                before = jnp.where(lane < wide, roll(before, 1, 0), before)
+                squares = squares + steepest(side, (value - before) * masks_y[region],
+                                             (row_ahead(turned[1, i]) - value) * ahead_y[region])
+                squares = squares + steepest(side, (value - turned[2, i]) * masks_z[region],
+                                             (turned[3, i] - value) * ahead_z[region]) + EPSILON
+                level[later, i] = value - TIME_STEP * field * (squares * lax.rsqrt(squares) - 1.0)
 
     for step in range(STEPS):
         sweep(step, step + 1, layers - 1 - step)
@@ -313,7 +325,7 @@
             table, table, table,
         ] + [buffer] * 4 + [
             pair(edge // 2), pair(slots), pair(slots), pair(3, slots), pair(3, slots),
-            pair(edge // 4), pair(edge // 4), pair(2, layers), pair(layers),
+            pair(edge // 4), pair(edge // 4), pair(2, layers), pair(layers), pair(4, layers),
             pltpu.SemaphoreType.DMA((3,)),
         ] + [pltpu.SemaphoreType.DMA((columns,))] * 4 + [pltpu.SemaphoreType.DMA((10,))] * 2,
         compiler_params=pltpu.CompilerParams(

time: 26.9 us -> 26.1 us (0.970)
  Pallas kernels: 26.1 us -> 25.2 us
    pallas_call x1, Pallas kernels: 26.1 us -> 25.2 us  [on_device(): pl.pallas_call(functools.partial(kernel, columns, groups), out_shape=jax....]
where the time goes in v3:
time: 26.1 us; the launch traced here: 25.9 us
  Pallas kernels  25.2 us (97%)
  local copies, waits for them, and re-layouts  0.71 us (3%)
    pallas_call x1, Pallas kernels, on_device(): pl.pallas_call(functools.partial(kernel, columns, groups), out_shape=jax....  25.2 us
    unnamed x1, local copies, waits for them, and re-layouts  0.71 us

profile of v3, /device:TPU:0, one launch (start us, length us, event | category | flops | bytes accessed | tf_op | source)
XLA Modules:
  0.0 25.9 jit_solution(3692910667825050006)
XLA Ops:
  0.0 25.2 %shard_map.37 = f32[8,8,8,128]{3,2,1,0:T(8,128)S(1)} custom-call(f32[8,8,8,128]{3,2,1,0:T(8,128)} %phi_hbm.1, s32[1,16]{1,0:T(1,128)} %counts_hbm.1, s32[6,1,512]{2,1,0:T(1,128)} %bitcast.1), custom_call_target="tpu_custom_call" | custom-call | tf_op jit(solution)/shard_map/pallas_call | solution.py:318
  25.2 0.7 %copy.5 = f32[8,8,8,128]{3,2,1,0:T(8,128)} copy(f32[8,8,8,128]{3,2,1,0:T(8,128)S(1)} %shard_map.37) | data formatting | bytes 524288

commit v4 on v3

--- a/solution.py
+++ b/solution.py
@@ -59,17 +59,13 @@
     ]
     for copy in fetch:
         copy.start()
-    for ref in (from_below, from_above, from_left, from_right):
-        ref[...] = jnp.zeros_like(ref)
-    for ref in (links_below, links_above):
-        ref[...] = jnp.full_like(ref, -1)
 
     barrier = pltpu.get_barrier_semaphore()
 
     def greet(**peer):
         pl.semaphore_signal(barrier, inc=1, device_id=peer, device_id_type=pl.DeviceIdType.MESH)
 
-    for d in distances:
+    for d in sorted(distances, key=lambda d: -min(d, columns - d)):
         greet(mem=lax.rem(me + d, columns))
     greetings = jnp.int32(columns - 1)
     for dg, there in across_grp:
@@ -86,10 +82,21 @@
             src_ref=source, dst_ref=target, send_sem=send, recv_sem=recv,
             device_id=peer, device_id_type=pl.DeviceIdType.MESH)
 
-    def begin_exchange(source, target, send, recv):
+    early = 2
+
+    def turn(i, favour):
+        if not favour:
+            return lax.rem(me + 1 + i, columns)
+        if i == 0:
+            return jnp.where(me == 0, 1, 0)
+        rest = early + lax.rem(me + columns - 3 * early + i + 1, columns - early)
+        return jnp.where(me < early, i + 1, 1 if i == 1 else rest)
+
+    def begin_exchange(source, target, send, recv, favour=False):
         started = []
-        for d in distances:
-            peer = lax.rem(me + d, columns)
+        for i in range(columns - 1):
+            peer = turn(i, favour)
+            d = lax.rem(peer - me + columns, columns)
             copy = remote(source.at[peer], target.at[me], send.at[d], recv.at[d], mem=peer)
             copy.start()
             started.append(copy)
@@ -137,6 +144,19 @@
         shift(1, has_below, has_above, remote(
             links_own, links_above, side_send.at[1], side_recv.at[1], grp=grp - 1)),
     ]
+
+    def blank(absent, *views):
+        @pl.when(jnp.logical_not(absent))
+        def _():
+            for ref, value in views:
+                ref[...] = jnp.full_like(ref, value)
+
+    blank(has_left, (from_left, 0.0))
+    blank(has_right, (from_right, 0.0))
+    for there, table, ref in ((has_below, links_below, from_below), (has_above, links_above, from_above)):
+        blank(there, (table, -1), (ref.at[1], 0.0))
+        blank(jnp.logical_and(there, has_left), (ref.at[0], 0.0))
+        blank(jnp.logical_and(there, has_right), (ref.at[2], 0.0))
 
     def arrival(dims, axis):
         entry = lax.broadcasted_iota(jnp.int32, dims, axis)
@@ -288,7 +308,7 @@
         final.append(jnp.where(z < edge, roll(one, -halo, 1), roll(two, edge - halo, 1)))
     back[...] = dot(depart, pieces(jnp.concatenate(final, axis=1), 0),
                     ((1,), (0,))).reshape(back.shape)
-    sent += begin_exchange(back, home, back_send, back_recv)
+    sent += begin_exchange(back, home, back_send, back_recv, True)
     end_exchange(back, home, back_send, back_recv)
 
     owned = dot(living, pieces(home[...].reshape(-1, home.shape[2]), 0), ((0,), (0,))).T

time: 26.1 us -> 26 us (level)
  no operation moved by 1% of the time
where the time goes in v4:
time: 26 us; the launch traced here: 25.8 us
  Pallas kernels  25.1 us (97%)
  local copies, waits for them, and re-layouts  0.71 us (3%)
    pallas_call x1, Pallas kernels, on_device(): pl.pallas_call(functools.partial(kernel, columns, groups), out_shape=jax....  25.1 us
    unnamed x1, local copies, waits for them, and re-layouts  0.71 us

profile of v4, /device:TPU:0, one launch (start us, length us, event | category | flops | bytes accessed | tf_op | source)
XLA Modules:
  0.0 25.8 jit_solution(17238040413597162571)
XLA Ops:
  0.0 25.1 %shard_map.37 = f32[8,8,8,128]{3,2,1,0:T(8,128)S(1)} custom-call(f32[8,8,8,128]{3,2,1,0:T(8,128)} %phi_hbm.1, s32[1,16]{1,0:T(1,128)} %counts_hbm.1, s32[6,1,512]{2,1,0:T(1,128)} %bitcast.1), custom_call_target="tpu_custom_call" | custom-call | tf_op jit(solution)/shard_map/pallas_call | solution.py:338
  25.1 0.7 %copy.5 = f32[8,8,8,128]{3,2,1,0:T(8,128)} copy(f32[8,8,8,128]{3,2,1,0:T(8,128)S(1)} %shard_map.37) | data formatting | bytes 524288

commit v5 on v4

--- a/solution.py
+++ b/solution.py
@@ -36,7 +36,7 @@
     columns, groups, phi_hbm, counts_hbm, links_hbm, out_ref,
     phi_ref, counts_ref, links_own, links_below, links_above,
     leave, land, back, home, pack, up, down, from_below, from_above, from_left, from_right,
-    level, sign, turned, in_sem, out_send, out_recv, back_send, back_recv, side_send, side_recv,
+    level, sign, turned, slopes, in_sem, out_send, out_recv, back_send, back_recv, side_send, side_recv,
 ):
     edge = phi_ref.shape[0]
     own_slots = phi_ref.shape[3]
@@ -270,30 +270,30 @@
                 for i in range(low, high):
                     turned[k, i] = roll(level[now, i], shift_by, 1)
 
+            def across(j):
+                change = level[now, j] - level[now, j - 1]
+                if j == halo:
+                    change = change * link_x[0]
+                elif j == halo + edge:
+                    change = change * link_x[1]
+                return change
+
+            gap = across(low)
+            for i in range(low, high):
+                ahead = across(i + 1)
+                slopes[i] = steepest(jnp.where(sign[i] > 0, 1.0, -1.0), gap, ahead)
+                gap = ahead
+
         @pl.when(always)
         def _():
-            gap = None
             for i in range(low, high):
                 region = 0 if i < halo else (1 if i < halo + edge else 2)
                 value, field = level[now, i], sign[i]
                 side = jnp.where(field > 0, 1.0, -1.0)
-
-                def across(j):
-                    change = level[now, j] - level[now, j - 1]
-                    if j == halo:
-                        change = change * link_x[0]
-                    elif j == halo + edge:
-                        change = change * link_x[1]
-                    return change
-
-                gap = across(i) if gap is None else gap
-                ahead = across(i + 1)
-                squares = steepest(side, gap, ahead)
-                gap = ahead
                 before = turned[0, i]
                 before = jnp.where(lane < wide, roll(before, 1, 0), before)
-                squares = squares + steepest(side, (value - before) * masks_y[region],
-                                             (row_ahead(turned[1, i]) - value) * ahead_y[region])
+                squares = slopes[i] + steepest(side, (value - before) * masks_y[region],
+                                               (row_ahead(turned[1, i]) - value) * ahead_y[region])
                 squares = squares + steepest(side, (value - turned[2, i]) * masks_z[region],
                                              (turned[3, i] - value) * ahead_z[region]) + EPSILON
                 level[later, i] = value - TIME_STEP * field * (squares * lax.rsqrt(squares) - 1.0)
@@ -302,10 +302,9 @@
         sweep(step, step + 1, layers - 1 - step)
 
     last = STEPS % 2
-    final = []
-    for pair in range(edge // 2):
-        one, two = level[last, halo + 2 * pair], level[last, halo + 2 * pair + 1]
-        final.append(jnp.where(z < edge, roll(one, -halo, 1), roll(two, edge - halo, 1)))
+    low_half = [roll(level[last, halo + 2 * p], -halo, 1) for p in range(edge // 2)]
+    high_half = [roll(level[last, halo + 2 * p + 1], edge - halo, 1) for p in range(edge // 2)]
+    final = [jnp.where(z < edge, one, two) for one, two in zip(low_half, high_half)]
     back[...] = dot(depart, pieces(jnp.concatenate(final, axis=1), 0),
                     ((1,), (0,))).reshape(back.shape)
     sent += begin_exchange(back, home, back_send, back_recv, True)
@@ -345,7 +344,7 @@
             table, table, table,
         ] + [buffer] * 4 + [
             pair(edge // 2), pair(slots), pair(slots), pair(3, slots), pair(3, slots),
-            pair(edge // 4), pair(edge // 4), pair(2, layers), pair(layers), pair(4, layers),
+            pair(edge // 4), pair(edge // 4), pair(2, layers), pair(layers), pair(4, layers), pair(layers),
             pltpu.SemaphoreType.DMA((3,)),
         ] + [pltpu.SemaphoreType.DMA((columns,))] * 4 + [pltpu.SemaphoreType.DMA((10,))] * 2,
         compiler_params=pltpu.CompilerParams(

time: 26 us -> 26 us (level)
  no operation moved by 1% of the time
where the time goes in v5:
time: 26 us; the launch traced here: 25.9 us
  Pallas kernels  25.2 us (97%)
  local copies, waits for them, and re-layouts  0.71 us (3%)
    pallas_call x1, Pallas kernels, on_device(): pl.pallas_call(functools.partial(kernel, columns, groups), out_shape=jax....  25.2 us
    unnamed x1, local copies, waits for them, and re-layouts  0.71 us

profile of v5, /device:TPU:0, one launch (start us, length us, event | category | flops | bytes accessed | tf_op | source)
XLA Modules:
  0.0 25.9 jit_solution(6894084400899525045)
XLA Ops:
  0.0 25.2 %shard_map.37 = f32[8,8,8,128]{3,2,1,0:T(8,128)S(1)} custom-call(f32[8,8,8,128]{3,2,1,0:T(8,128)} %phi_hbm.1, s32[1,16]{1,0:T(1,128)} %counts_hbm.1, s32[6,1,512]{2,1,0:T(1,128)} %bitcast.1), custom_call_target="tpu_custom_call" | custom-call | tf_op jit(solution)/shard_map/pallas_call | solution.py:337
  25.2 0.7 %copy.5 = f32[8,8,8,128]{3,2,1,0:T(8,128)} copy(f32[8,8,8,128]{3,2,1,0:T(8,128)S(1)} %shard_map.37) | data formatting | bytes 524288
